TPU v7x, 128 devices: a whole 4x4x4 slice. The times are simulated.
128 devices in a mesh: gx: 8 (over x, z_lo), gy: 16 (over z_hi, y, core).
Axes of the slice: x: 4, y: 4, z: 4 (z_hi: 2, z_lo: 2; z = z_hi * 2 + z_lo), core: 2. Of those that a mesh axis runs over, the one named last changes fastest.
Arguments:
- velocity: float32 [2, 4096, 8192], P(None, 'gx', 'gy'), may hold values from -3 to 3
- stress: float32 [3, 4096, 8192], P(None, 'gx', 'gy'), may hold values from -3 to 3
- strength: float32 [4096, 8192], P('gx', 'gy'), may hold values from 0.5 to 4
- ice_mass: float32 [4096, 8192], P('gx', 'gy'), may hold values from 0.3 to 20, as said below
- wind_stress: float32 [2, 4096, 8192], P(None, 'gx', 'gy'), may hold values from -6 to 6
- current: float32 [2, 4096, 8192], P(None, 'gx', 'gy'), may hold values from -3 to 3
- ice_mask: int32 [4096, 8192], P('gx', 'gy'), may hold values from 0 to 1, as said below
- open_water: int32 [4096, 8192], P('gx', 'gy'), may hold values 0 or 1
Outputs:
- new_velocity: float32 [2, 4096, 8192], P(None, 'gx', 'gy')
- new_stress: float32 [3, 4096, 8192], P(None, 'gx', 'gy')
- residual: float32 [], replicated
- kinetic_energy: float32 [], replicated
Inputs may be any that keep to these rules, and one draw needn't show every extreme that they name: `ice_mask`: 1 marks an ocean cell, 0 a land cell. `ice_mass`: positive everywhere.
All inputs are finite; a program needn't handle non-finite values. No bound on the sum of `open_water` on one device may be relied on, other than what follows from the above.
Results may differ from a plain program's by a relative error of at most 0.00002.
Values sent between devices are 32-bit elements; how exact they have to be, the bound alone decides.
A program may use at most 128 MiB of HBM per device.

v0:
```python
import functools

import jax
import jax.numpy as jnp
from jax import lax
from jax.experimental import pallas as pl
from jax.experimental.pallas import tpu as pltpu
from jax.sharding import Mesh
from jax.sharding import PartitionSpec as P

ITERS = 4
GX = ("gx_0", "gx_1")
GY = ("gy_0", "gy_1", "gy_2")
AXES = GX + GY

relax_rate = 0.8
ecc_square = 4.0
delta_floor = 0.05
time_step = 0.5
drag_coef = 1.0
coriolis = 0.3

F32 = jnp.float32
LANES = 128
CHUNKS = 8
FIELDS = 11
U, V, A, B, T, PR, AL, BE, IN, KU, KV = range(FIELDS)
SWAPPED = (V, U, B, A, T, PR, AL, BE, IN, KV, KU)
STRIP_ROWS = 56
TOP_HALO, TOP_OWN, BOT_OWN, BOT_HALO = 8, 16, 32, 40

DECAY = 1.0 / (1.0 + relax_rate)
FLOOR = 4.0 * delta_floor * delta_floor


def lane_ids():
    return lax.broadcasted_iota(jnp.int32, (8, LANES), 1)


def row_ids():
    return lax.broadcasted_iota(jnp.int32, (8, LANES), 0)


def from_left(blocks):
    first = lane_ids() == 0
    rolled = [pltpu.roll(x, 1, 1) for x in blocks]
    return [jnp.where(first, rolled[b - 1], rolled[b]) for b in range(len(blocks))]


def from_right(blocks):
    last = lane_ids() == LANES - 1
    rolled = [pltpu.roll(x, LANES - 1, 1) for x in blocks]
    count = len(blocks)
    return [jnp.where(last, rolled[(b + 1) % count], rolled[b]) for b in range(count)]


class Domain:
    def __init__(self, blocks, get):
        self.blocks = blocks
        self.get = get

    def read(self, field, level, row):
        ref = self.get(field, level)
        return [ref[b, pl.ds(row, 8), :] for b in range(self.blocks)]

    def write(self, field, level, row, values):
        ref = self.get(field, level)
        for b in range(self.blocks):
            ref[b, pl.ds(row, 8), :] = values[b]


def stress_phase(dom, level, row):
    n = dom.blocks
    u, um = dom.read(U, level, row), dom.read(U, level, row - 1)
    v, vm = dom.read(V, level, row), dom.read(V, level, row - 1)
    pr = dom.read(PR, 0, row)
    sa, sb, st = (dom.read(f, level, row) for f in (A, B, T))
    m1, m2, m3, m4 = [], [], [], []
    for b in range(n):
        du, su = u[b] - um[b], u[b] + um[b]
        dv, sv = v[b] - vm[b], v[b] + vm[b]
        m1.append(du + sv)
        m2.append(du - sv)
        m3.append(su + dv)
        m4.append(su - dv)
    l1, l2, l4 = from_left(m1), from_left(m2), from_left(m4)
    na, nb, nt = [], [], []
    for b in range(n):
        div = m1[b] + l2[b]
        ten = m2[b] + l1[b]
        she = m3[b] - l4[b]
        ten4, she4 = 0.25 * ten, 0.25 * she
        rate = lax.rsqrt((div * div + FLOOR) + (ten * ten4 + she * she4))
        vis = pr[b] * rate
        e1 = vis * div - pr[b]
        e2 = vis * ten4
        na.append(DECAY * sa[b] + (e1 + e2))
        nb.append(DECAY * sb[b] + (e1 - e2))
        nt.append(DECAY * st[b] + vis * she4)
    dom.write(A, level + 1, row, na)
    dom.write(B, level + 1, row, nb)
    dom.write(T, level + 1, row, nt)
    return na, nb, nt


def velocity_phase(dom, level, row):
    n = dom.blocks
    sa, sap = dom.read(A, level + 1, row), dom.read(A, level + 1, row + 1)
    sb, sbp = dom.read(B, level + 1, row), dom.read(B, level + 1, row + 1)
    st, stp = dom.read(T, level + 1, row), dom.read(T, level + 1, row + 1)
    e, g, h, j = [], [], [], []
    for b in range(n):
        da, sumt = sap[b] - sa[b], stp[b] + st[b]
        dt, sumb = stp[b] - st[b], sbp[b] + sb[b]
        e.append(da + sumt)
        g.append(da - sumt)
        h.append(dt + sumb)
        j.append(dt - sumb)
    re, rh = from_right(e), from_right(h)
    u, v = dom.read(U, level, row), dom.read(V, level, row)
    al, be, inert = (dom.read(f, 0, row) for f in (AL, BE, IN))
    ku, kv = dom.read(KU, 0, row), dom.read(KV, 0, row)
    nu, nv = [], []
    for b in range(n):
        ru = inert[b] * u[b] + (re[b] + g[b]) + ku[b]
        rv = inert[b] * v[b] + (rh[b] + j[b]) + kv[b]
        nu.append(al[b] * ru + be[b] * rv)
        nv.append(al[b] * rv - be[b] * ru)
    dom.write(U, level + 1, row, nu)
    dom.write(V, level + 1, row, nv)
    return u, v, nu, nv, inert


def square_sums(phase, keep):
    res, kin = None, None
    for u, v, nu, nv, inert, mask in zip(*phase, keep):
        if mask is False:
            continue
        du, dv = nu - u, nv - v
        r = du * du + dv * dv
        k = inert * (nu * nu + nv * nv)
        if mask is not None:
            r, k = jnp.where(mask, r, 0.0), jnp.where(mask, k, 0.0)
        res = r if res is None else res + r
        kin = k if kin is None else kin + k
    return res, kin


def wavefront(tiles, phases, carry, arrive=None):
    depth = max(lag for lag, _ in phases)

    def step(t, carry, active):
        if arrive is not None and active[0][0] == 0:
            arrive(t)
        for lag, phase in reversed(active):
            carry = phase(t - lag, carry)
        return carry

    for t in range(depth):
        carry = step(t, carry, [p for p in phases if p[0] <= t])
    carry = lax.fori_loop(depth, tiles, lambda t, c: step(t, c, phases), carry)
    for t in range(tiles, tiles + depth):
        carry = step(t, carry, [p for p in phases if t - p[0] < tiles])
    return carry


def main_kernel(
    vel, stress, strength, mass, wind, current, mask, water,
    out_vel, out_str, out_sum,
    uv0, str_in, strength_in, mass_in, wind_in, cur_in, mask_in, water_in,
    uv1, uv2, uv3, uv4, s0, s1, s2, s3, s4, coef,
    packed, rows0, rows_uv, rows_s, cols0, cols_uv, cols_s, turned,
    in_sem, send_sem, recv_sem,
):
    nrow, ncol = mass.shape
    nblk = ncol // LANES
    tiles = nrow // 8
    per = nrow // CHUNKS
    row_blks = nrow // LANES
    gx, gy = lax.axis_index(GX), lax.axis_index(GY)
    ngx, ngy = lax.axis_size(GX), lax.axis_size(GY)

    def copies(c):
        r = pl.ds(c * per, per)
        out = []
        for b in range(nblk):
            out.append((vel.at[:, r, b * LANES : (b + 1) * LANES], uv0.at[:, b, pl.ds(c * per + 8, per), :]))
        for src, dst in ((stress, str_in), (wind, wind_in), (current, cur_in)):
            out.append((src.at[:, r, :], dst.at[:, r, :]))
        for src, dst in ((strength, strength_in), (mass, mass_in), (mask, mask_in), (water, water_in)):
            out.append((src.at[r, :], dst.at[r, :]))
        return [pltpu.make_async_copy(s, d, in_sem.at[i, c]) for i, (s, d) in enumerate(out)]

    for c in [0, CHUNKS - 1] + list(range(1, CHUNKS - 1)):
        for copy in copies(c):
            copy.start()

    def peer(axis, step):
        if axis == 0:
            x, y = lax.rem(gx + step + ngx, ngx), gy
        else:
            x, y = gx, lax.rem(gy + step + ngy, ngy)
        ids = {}
        for names, index in ((GX, x), (GY, y)):
            for name in reversed(names):
                size = lax.axis_size(name)
                ids[name] = lax.rem(index, size)
                index = lax.div(index, size)
        return tuple(ids[name] for name in AXES)

    barrier = pltpu.get_barrier_semaphore()
    for axis in (0, 1):
        for step in (-1, 1):
            pl.semaphore_signal(barrier, 1, device_id=peer(axis, step), device_id_type=pl.DeviceIdType.MESH)

    def prologue(row, b):
        r, l = pl.ds(row, 8), slice(b * LANES, (b + 1) * LANES)
        ice = mask_in[r, l] > water_in[r, l]
        m = mass_in[r, l]
        diag, turn = m * (1.0 / time_step) + drag_coef, m * coriolis
        inv = jnp.where(ice, 0.25 / (diag * diag + turn * turn), 0.0)
        first, second = str_in[0, r, l], str_in[1, r, l]
        pres = jnp.where(ice, strength_in[r, l] * (relax_rate * DECAY), 0.0)
        at = pl.ds(row + 8, 8)
        return [
            uv0[0, b, at, :], uv0[1, b, at, :],
            first + second, first - second, 2.0 * str_in[2, r, l],
            pres, diag * inv, turn * inv, m * (4.0 / time_step),
            4.0 * (wind_in[0, r, l] + drag_coef * cur_in[0, r, l]),
            4.0 * (wind_in[1, r, l] + drag_coef * cur_in[1, r, l]),
        ]

    for c in (0, CHUNKS - 1):
        for copy in copies(c):
            copy.wait()
    for row, at in ((0, TOP_OWN), (nrow - 8, BOT_OWN)):
        for b in range(nblk):
            for f, x in enumerate(prologue(row, b)):
                rows0[f, b, pl.ds(at, 8), :] = x

    def exchange(strip, axis):
        out = []
        for way, (step, src, dst) in enumerate(((-1, TOP_OWN, BOT_HALO), (1, BOT_OWN + 4, TOP_HALO + 4))):
            out.append(
                pltpu.make_async_remote_copy(
                    src_ref=strip.at[:, :, pl.ds(src, 4), :],
                    dst_ref=strip.at[:, :, pl.ds(dst, 4), :],
                    send_sem=send_sem.at[axis, way],
                    recv_sem=recv_sem.at[axis, way],
                    device_id=peer(axis, step),
                    device_id_type=pl.DeviceIdType.MESH,
                )
            )
        return out

    def no_outside(strip, index, count):
        @pl.when(index == 0)
        def _():
            strip[:, :, TOP_HALO : TOP_HALO + 8, :] = jnp.zeros_like(strip[:, :, TOP_HALO : TOP_HALO + 8, :])

        @pl.when(index == count - 1)
        def _():
            strip[:, :, BOT_HALO : BOT_HALO + 8, :] = jnp.zeros_like(strip[:, :, BOT_HALO : BOT_HALO + 8, :])

    pl.semaphore_wait(barrier, 4)
    row_copies = exchange(rows0, 0)
    for copy in row_copies:
        copy.start()

    uvs, ss = (uv0, uv1, uv2, uv3, uv4), (s0, s1, s2, s3, s4)

    def main_get(field, level):
        if field in (U, V):
            return uvs[level].at[field]
        if field in (A, B, T):
            return ss[level].at[field - A]
        return coef.at[field - PR]

    main = Domain(nblk, main_get)
    lane = lane_ids()

    def pack(tile_fields, shift):
        out = None
        for slot, f in enumerate(SWAPPED):
            x = tile_fields[f]
            by = (8 * slot + shift) % LANES
            x = pltpu.roll(x, by, 1) if by else x
            out = x if out is None else jnp.where(lane < 8 * slot, out, x)
        return out

    def arrive(tile):
        if isinstance(tile, int):
            c = tile * 8 // per
            if tile * 8 % per == 0 and c not in (0, CHUNKS - 1):
                for copy in copies(c):
                    copy.wait()
        else:
            c = lax.div(tile, per // 8)

            @pl.when((lax.rem(tile, per // 8) == 0) & (c > 0) & (c < CHUNKS - 1))
            def _():
                for copy in copies(c):
                    copy.wait()

    def prepare(tile, carry):
        row = tile * 8 if isinstance(tile, int) else pl.multiple_of(tile * 8, 8)
        at = row + 8
        for b in range(nblk):
            fields = prologue(row, b)
            for f in (A, B, T):
                s0[f - A, b, pl.ds(at, 8), :] = fields[f]
            for f in range(PR, FIELDS):
                coef[f - PR, b, pl.ds(at, 8), :] = fields[f]
            if b == 0:
                packed[0, pl.ds(row, 8), :] = pack(fields, 0)
            if b == nblk - 1:
                packed[1, pl.ds(row, 8), :] = pack(fields, 8)
        return carry

    def at_row(tile):
        return tile * 8 + 8 if isinstance(tile, int) else pl.multiple_of(tile * 8 + 8, 8)

    def stress_at(level):
        def phase(tile, carry):
            stress_phase(main, level, at_row(tile))
            return carry

        return phase

    def velocity_at(level):
        def phase(tile, carry):
            velocity_phase(main, level, at_row(tile))
            return carry

        return phase

    def put_stress(tile, blocks):
        na, nb, nt = blocks
        r = pl.ds(tile * 8, 8) if isinstance(tile, int) else pl.ds(pl.multiple_of(tile * 8, 8), 8)
        for b in range(nblk):
            l = slice(b * LANES, (b + 1) * LANES)
            out_str[0, r, l] = 0.5 * (na[b] + nb[b])
            out_str[1, r, l] = 0.5 * (na[b] - nb[b])
            out_str[2, r, l] = 0.5 * nt[b]

    def last_stress(tile, carry):
        put_stress(tile, stress_phase(main, ITERS - 1, at_row(tile)))
        return carry

    inner = [None] * nblk
    inner[0] = lane >= 4
    inner[nblk - 1] = lane < LANES - 4

    def last_velocity(tile, carry):
        u, v, nu, nv, inert = velocity_phase(main, ITERS - 1, at_row(tile))
        r = pl.ds(tile * 8, 8) if isinstance(tile, int) else pl.ds(pl.multiple_of(tile * 8, 8), 8)
        for b in range(nblk):
            l = slice(b * LANES, (b + 1) * LANES)
            out_vel[0, r, l] = nu[b]
            out_vel[1, r, l] = nv[b]
        res, kin = square_sums((u, v, nu, nv, inert), inner)
        keep = jnp.int32(0) + row_ids() + tile * 8
        good = (keep >= 4) & (keep < nrow - 4)
        return carry[0] + jnp.where(good, res, 0.0), carry[1] + jnp.where(good, kin, 0.0)

    zero = jnp.zeros((8, LANES), F32)
    wavefront(
        tiles,
        [(0, prepare), (1, stress_at(0)), (3, velocity_at(0)), (4, stress_at(1)), (6, velocity_at(1))],
        0,
        arrive,
    )

    for copy in row_copies:
        copy.wait()
    no_outside(rows0, gx, ngx)
    for side, b, shift in ((0, 0, 0), (1, nblk - 1, 8)):
        for at, to in ((BOT_HALO, nrow), (TOP_HALO, nrow + LANES - 8)):
            packed[side, pl.ds(to, 8), :] = pack([rows0[f, b, pl.ds(at, 8), :] for f in range(FIELDS)], shift)
        for blk in range(row_blks + 1):
            flat = packed[side, pl.ds(blk * LANES, LANES), :].T
            for f in range(FIELDS):
                x = flat[8 * f : 8 * f + 8, :]
                cols0[f, blk, pl.ds((TOP_OWN, BOT_OWN)[side], 8), :] = -x if f == BE else x
    col_copies = exchange(cols0, 1)
    for copy in col_copies:
        copy.start()

    sums = wavefront(
        tiles,
        [(0, stress_at(2)), (2, velocity_at(2)), (3, last_stress), (5, last_velocity)],
        (zero, zero),
    )

    def strip_get(first, uv, s):
        def get(field, level):
            if level == 0:
                return first.at[field]
            return uv.at[level - 1, field] if field in (U, V) else s.at[level - 1, field - A]

        return get

    def sweep_strip(dom):
        own = {}
        for level in range(ITERS):
            for at in (TOP_HALO, TOP_OWN, BOT_OWN, BOT_HALO):
                stress_phase(dom, level, at)
            for at in (TOP_HALO, TOP_OWN, BOT_OWN, BOT_HALO):
                own[at] = velocity_phase(dom, level, at)
        return own

    def add(sums, more):
        return sums[0] + more[0], sums[1] + more[1]

    sub = row_ids()
    row_dom = Domain(nblk, strip_get(rows0, rows_uv, rows_s))
    own = sweep_strip(row_dom)
    for at, row, good in ((TOP_OWN, 0, sub < 4), (BOT_OWN, nrow - 8, sub >= 4)):
        keep = [good if m is None else good & m for m in inner]
        sums = add(sums, square_sums(own[at], keep))
        _, _, nu, nv, _ = own[at]
        sa, sb, st = (row_dom.read(f, ITERS, at) for f in (A, B, T))
        for b in range(nblk):
            r, l = pl.ds(row, 8), slice(b * LANES, (b + 1) * LANES)
            for ref, i, x in (
                (out_vel, 0, nu[b]), (out_vel, 1, nv[b]),
                (out_str, 0, 0.5 * (sa[b] + sb[b])), (out_str, 1, 0.5 * (sa[b] - sb[b])), (out_str, 2, 0.5 * st[b]),
            ):
                ref[i, r, l] = jnp.where(good, x, ref[i, r, l])

    for copy in col_copies:
        copy.wait()
    no_outside(cols0, gy, ngy)
    col_dom = Domain(row_blks + 1, strip_get(cols0, cols_uv, cols_s))
    own = sweep_strip(col_dom)
    for side, (at, good) in enumerate(((TOP_OWN, sub < 4), (BOT_OWN, sub >= 4))):
        sums = add(sums, square_sums(own[at], [good] * row_blks + [False]))
        _, _, nu, nv, _ = own[at]
        sa, sb, st = (col_dom.read(f, ITERS, at) for f in (A, B, T))
        for blk in range(row_blks):
            values = (
                nv[blk], nu[blk],
                0.5 * (sb[blk] + sa[blk]), 0.5 * (sb[blk] - sa[blk]), 0.5 * st[blk],
            )
            for i, x in enumerate(values):
                turned[blk, pl.ds(40 * side + 8 * i, 8), :] = x
    for blk in range(row_blks):
        packed[0, pl.ds(blk * LANES, LANES), :] = turned[blk].T

    def merge(tile, carry):
        r = pl.ds(pl.multiple_of(tile * 8, 8), 8)
        x = packed[0, r, :]
        places = [((out_vel, i) if i < 2 else (out_str, i - 2)) for i in range(5)]
        first, last = slice(0, LANES), slice(ncol - LANES, ncol)
        new = []
        for i, (ref, at) in enumerate(places):
            left = pltpu.roll(x, (LANES - 8 * i) % LANES, 1) if i else x
            right = pltpu.roll(x, (LANES - 8 - 40 - 8 * i) % LANES, 1)
            if first == last:
                new.append((ref, at, first, jnp.where(lane < 4, left, jnp.where(lane >= LANES - 4, right, ref[at, r, first]))))
            else:
                new.append((ref, at, first, jnp.where(lane < 4, left, ref[at, r, first])))
                new.append((ref, at, last, jnp.where(lane >= LANES - 4, right, ref[at, r, last])))
        for ref, at, l, value in new:
            ref[at, r, l] = value
        return carry

    lax.fori_loop(0, tiles, merge, 0, unroll=4)
    out_sum[0] = sums[0]
    out_sum[1] = sums[1]


def per_device(velocity, stress, strength, ice_mass, wind_stress, current, ice_mask, open_water):
    nrow, ncol = ice_mass.shape
    nblk = ncol // LANES
    row_blks = nrow // LANES
    pad = nrow + 16
    vmem = pltpu.VMEM
    any_spec = pl.BlockSpec(memory_space=pl.ANY)
    vmem_spec = pl.BlockSpec(memory_space=pltpu.VMEM)
    new_velocity, new_stress, parts = pl.pallas_call(
        main_kernel,
        out_shape=(
            jax.ShapeDtypeStruct(velocity.shape, F32),
            jax.ShapeDtypeStruct(stress.shape, F32),
            jax.ShapeDtypeStruct((2, 8, LANES), F32),
        ),
        in_specs=[any_spec] * 8,
        out_specs=(vmem_spec, vmem_spec, vmem_spec),
        scratch_shapes=[
            vmem((2, nblk, pad, LANES), F32),
            vmem((3, nrow, ncol), F32),
            vmem((nrow, ncol), F32),
            vmem((nrow, ncol), F32),
            vmem((2, nrow, ncol), F32),
            vmem((2, nrow, ncol), F32),
            vmem((nrow, ncol), jnp.int32),
            vmem((nrow, ncol), jnp.int32),
        ]
        + [vmem((2, nblk, pad, LANES), F32)] * ITERS
        + [vmem((3, nblk, pad, LANES), F32)] * (ITERS + 1)
        + [
            vmem((FIELDS - PR, nblk, pad, LANES), F32),
            vmem((2, nrow + LANES, LANES), F32),
            vmem((FIELDS, nblk, STRIP_ROWS, LANES), F32),
            vmem((ITERS, 2, nblk, STRIP_ROWS, LANES), F32),
            vmem((ITERS, 3, nblk, STRIP_ROWS, LANES), F32),
            vmem((FIELDS, row_blks + 1, STRIP_ROWS, LANES), F32),
            vmem((ITERS, 2, row_blks + 1, STRIP_ROWS, LANES), F32),
            vmem((ITERS, 3, row_blks + 1, STRIP_ROWS, LANES), F32),
            vmem((row_blks, LANES, LANES), F32),
            pltpu.SemaphoreType.DMA((nblk + 7, CHUNKS)),
            pltpu.SemaphoreType.DMA((2, 2)),
            pltpu.SemaphoreType.DMA((2, 2)),
        ],
        compiler_params=pltpu.CompilerParams(
            collective_id=0, has_side_effects=True, vmem_limit_bytes=62 * 1024 * 1024
        ),
        name="subcycles",
    )(velocity, stress, strength, ice_mass, wind_stress, current, ice_mask, open_water)
    totals = lax.psum(jnp.sum(parts, axis=(1, 2)), AXES)
    cells = nrow * lax.axis_size(GX) * ncol * lax.axis_size(GY)
    return (
        new_velocity,
        new_stress,
        totals[0] / cells,
        totals[1] * (0.5 * time_step / 4.0) / cells,
    )


def solution(mesh):
    split = Mesh(mesh.devices.reshape(4, 2, 2, 4, 2), AXES)
    return jax.shard_map(
        per_device,
        mesh=split,
        in_specs=(
            P(None, GX, GY),
            P(None, GX, GY),
            P(GX, GY),
            P(GX, GY),
            P(None, GX, GY),
            P(None, GX, GY),
            P(GX, GY),
            P(GX, GY),
        ),
        out_specs=(P(None, GX, GY), P(None, GX, GY), P(), P()),
        check_vma=False,
    )
```

profile of v0, /device:TPU:1, one launch (start us, length us, event | category | flops | bytes accessed | tf_op | source)
XLA Modules:
  0.0 108.6 jit_solution(2490634736175748606)
XLA Ops:
  0.6 31.9 %subcycles.1 = (f32[2,512,512]{2,1,0:T(8,128)}, f32[3,512,512]{2,1,0:T(8,128)}, f32[2,8,128]{2,1,0:T(8,128)}) custom-call(f32[2,512,512]{2,1,0:T(8,128)} %vel.1, f32[3,512,512]{2,1,0:T(8,128)} %stress.1, f32[512,512]{1,0:T(8,128)} %strength.1, f32[512,512]{1,0:T(8,128)} %mass.1, f32[2,512,512]{2,1,0:T(8,128)} %wind.1, f32[2,512,512]{2,1,0:T(8,128)} %current.1, ...), custom_call_target="tpu_custom_call" | custom-call | tf_op jit(solution)/shard_map/subcycles/pallas_call | solution.py:481
  32.6 0.8 reduce_sum.9
  33.4 66.2 %psum.7 = f32[2]{0:T(128)S(1)} all-reduce(f32[2]{0:T(128)S(1)} %reduce_sum.9), channel_id=1, replica_groups=mesh['gx_0'=4,'gx_1'=2,'gy_0'=2,'gy_1'=4,'gy_2'=2] {'gx_0','gx_1','gy_0'..., use_global_device_ids=true, to_apply=%region_1.0 | all-reduce | flops 2 | bytes 16 | tf_op jit(solution)/shard_map/psum | solution.py:521
  99.6 0.6 fusion
  101.5 0.0 copy-start
  101.5 3.2 %copy.14 = f32[2,512,512]{2,1,0:T(8,128)} copy(f32[2,512,512]{2,1,0:T(8,128)} %get-tuple-element.16) | data formatting | bytes 4194304
  104.7 0.0 copy-done
  104.7 1.7 %copy.15 = f32[3,512,512]{2,1,0:T(8,128)} copy(f32[3,512,512]{2,1,0:T(8,128)S(1)} %copy-done) | data formatting | bytes 6291456
Async XLA Ops:
  101.5 3.3 %copy-start = (f32[3,512,512]{2,1,0:T(8,128)S(1)}, f32[3,512,512]{2,1,0:T(8,128)}, u32[]{:S(2)}) copy-start(f32[3,512,512]{2,1,0:T(8,128)} %get-tuple-element.17) | copy-start | bytes 9437188
where the time goes:
time: 109 us
  blocking collectives  66.2 us (61%)
  Pallas kernels  31.9 us (29%)
  local copies, waits for them, and re-layouts  5.49 us (5%)
  between operations  4.21 us (4%)
    psum x1, blocking collectives, per_device(): totals = lax.psum(jnp.sum(parts, axis=(1, 2)), AXES)  66.2 us
    pallas_call x1, Pallas kernels, per_device(): pl.pallas_call(main_kernel, out_shape=(jax.ShapeDtypeStruct(velocity.shap...  31.9 us
    unnamed x4, local copies, waits for them, and re-layouts  4.91 us

commit v1 on v0

--- a/solution.py
+++ b/solution.py
@@ -23,50 +23,53 @@
 F32 = jnp.float32
 LANES = 128
 CHUNKS = 8
+AHEAD = 3
+TALL = 16
 FIELDS = 11
 U, V, A, B, T, PR, AL, BE, IN, KU, KV = range(FIELDS)
 SWAPPED = (V, U, B, A, T, PR, AL, BE, IN, KV, KU)
-STRIP_ROWS = 56
-TOP_HALO, TOP_OWN, BOT_OWN, BOT_HALO = 8, 16, 32, 40
+STRIP_ROWS = 40
+TOP_HALO, TOP_OWN, BOT_OWN, BOT_HALO = 8, 12, 20, 28
 
 DECAY = 1.0 / (1.0 + relax_rate)
 FLOOR = 4.0 * delta_floor * delta_floor
 
 
-def lane_ids():
-    return lax.broadcasted_iota(jnp.int32, (8, LANES), 1)
-
-
-def row_ids():
-    return lax.broadcasted_iota(jnp.int32, (8, LANES), 0)
+def lane_ids(height=8):
+    return lax.broadcasted_iota(jnp.int32, (height, LANES), 1)
+
+
+def row_ids(height=8):
+    return lax.broadcasted_iota(jnp.int32, (height, LANES), 0)
 
 
 def from_left(blocks):
-    first = lane_ids() == 0
+    first = lane_ids(blocks[0].shape[0]) == 0
     rolled = [pltpu.roll(x, 1, 1) for x in blocks]
     return [jnp.where(first, rolled[b - 1], rolled[b]) for b in range(len(blocks))]
 
 
 def from_right(blocks):
-    last = lane_ids() == LANES - 1
+    last = lane_ids(blocks[0].shape[0]) == LANES - 1
     rolled = [pltpu.roll(x, LANES - 1, 1) for x in blocks]
     count = len(blocks)
     return [jnp.where(last, rolled[(b + 1) % count], rolled[b]) for b in range(count)]
 
 
 class Domain:
-    def __init__(self, blocks, get):
+    def __init__(self, blocks, get, height=8):
         self.blocks = blocks
+        self.height = height
         self.get = get
 
     def read(self, field, level, row):
         ref = self.get(field, level)
-        return [ref[b, pl.ds(row, 8), :] for b in range(self.blocks)]
+        return [ref[b, pl.ds(row, self.height), :] for b in range(self.blocks)]
 
     def write(self, field, level, row, values):
         ref = self.get(field, level)
         for b in range(self.blocks):
-            ref[b, pl.ds(row, 8), :] = values[b]
+            ref[b, pl.ds(row, self.height), :] = values[b]
 
 
 def stress_phase(dom, level, row):
@@ -166,15 +169,15 @@
 
 def main_kernel(
     vel, stress, strength, mass, wind, current, mask, water,
-    out_vel, out_str, out_sum,
+    out_vel, out_str, out_res, out_kin,
     uv0, str_in, strength_in, mass_in, wind_in, cur_in, mask_in, water_in,
     uv1, uv2, uv3, uv4, s0, s1, s2, s3, s4, coef,
     packed, rows0, rows_uv, rows_s, cols0, cols_uv, cols_s, turned,
-    in_sem, send_sem, recv_sem,
+    gather_x, gather_y, in_sem, send_sem, recv_sem, sum_send, sum_recv,
 ):
     nrow, ncol = mass.shape
     nblk = ncol // LANES
-    tiles = nrow // 8
+    tiles = nrow // TALL
     per = nrow // CHUNKS
     row_blks = nrow // LANES
     gx, gy = lax.axis_index(GX), lax.axis_index(GY)
@@ -191,7 +194,7 @@
             out.append((src.at[r, :], dst.at[r, :]))
         return [pltpu.make_async_copy(s, d, in_sem.at[i, c]) for i, (s, d) in enumerate(out)]
 
-    for c in [0, CHUNKS - 1] + list(range(1, CHUNKS - 1)):
+    for c in [0, CHUNKS - 1] + list(range(1, AHEAD)):
         for copy in copies(c):
             copy.start()
 
@@ -209,19 +212,19 @@
         return tuple(ids[name] for name in AXES)
 
     barrier = pltpu.get_barrier_semaphore()
-    for axis in (0, 1):
-        for step in (-1, 1):
+    for axis, count in ((0, ngx), (1, ngy)):
+        for step in range(1, count):
             pl.semaphore_signal(barrier, 1, device_id=peer(axis, step), device_id_type=pl.DeviceIdType.MESH)
 
-    def prologue(row, b):
-        r, l = pl.ds(row, 8), slice(b * LANES, (b + 1) * LANES)
+    def prologue(row, b, height):
+        r, l = pl.ds(row, height), slice(b * LANES, (b + 1) * LANES)
         ice = mask_in[r, l] > water_in[r, l]
         m = mass_in[r, l]
         diag, turn = m * (1.0 / time_step) + drag_coef, m * coriolis
         inv = jnp.where(ice, 0.25 / (diag * diag + turn * turn), 0.0)
         first, second = str_in[0, r, l], str_in[1, r, l]
         pres = jnp.where(ice, strength_in[r, l] * (relax_rate * DECAY), 0.0)
-        at = pl.ds(row + 8, 8)
+        at = pl.ds(row + 8, height)
         return [
             uv0[0, b, at, :], uv0[1, b, at, :],
             first + second, first - second, 2.0 * str_in[2, r, l],
@@ -235,12 +238,12 @@
             copy.wait()
     for row, at in ((0, TOP_OWN), (nrow - 8, BOT_OWN)):
         for b in range(nblk):
-            for f, x in enumerate(prologue(row, b)):
+            for f, x in enumerate(prologue(row, b, 8)):
                 rows0[f, b, pl.ds(at, 8), :] = x
 
     def exchange(strip, axis):
         out = []
-        for way, (step, src, dst) in enumerate(((-1, TOP_OWN, BOT_HALO), (1, BOT_OWN + 4, TOP_HALO + 4))):
+        for way, (step, src, dst) in enumerate(((-1, TOP_OWN, BOT_HALO), (1, BOT_OWN + 4, TOP_HALO))):
             out.append(
                 pltpu.make_async_remote_copy(
                     src_ref=strip.at[:, :, pl.ds(src, 4), :],
@@ -256,13 +259,13 @@
     def no_outside(strip, index, count):
         @pl.when(index == 0)
         def _():
-            strip[:, :, TOP_HALO : TOP_HALO + 8, :] = jnp.zeros_like(strip[:, :, TOP_HALO : TOP_HALO + 8, :])
+            strip[:, :, TOP_HALO : TOP_HALO + 4, :] = jnp.zeros(strip.shape[:2] + (4, LANES), F32)
 
         @pl.when(index == count - 1)
         def _():
-            strip[:, :, BOT_HALO : BOT_HALO + 8, :] = jnp.zeros_like(strip[:, :, BOT_HALO : BOT_HALO + 8, :])
-
-    pl.semaphore_wait(barrier, 4)
+            strip[:, :, BOT_HALO : BOT_HALO + 4, :] = jnp.zeros(strip.shape[:2] + (4, LANES), F32)
+
+    pl.semaphore_wait(barrier, ngx + ngy - 2)
     row_copies = exchange(rows0, 0)
     for copy in row_copies:
         copy.start()
@@ -276,8 +279,9 @@
             return ss[level].at[field - A]
         return coef.at[field - PR]
 
-    main = Domain(nblk, main_get)
+    main = Domain(nblk, main_get, TALL)
     lane = lane_ids()
+    tall_lane = lane_ids(TALL)
 
     def pack(tile_fields, shift):
         out = None
@@ -285,40 +289,50 @@
             x = tile_fields[f]
             by = (8 * slot + shift) % LANES
             x = pltpu.roll(x, by, 1) if by else x
-            out = x if out is None else jnp.where(lane < 8 * slot, out, x)
+            out = x if out is None else jnp.where(lane_ids(x.shape[0]) < 8 * slot, out, x)
         return out
 
     def arrive(tile):
         if isinstance(tile, int):
-            c = tile * 8 // per
-            if tile * 8 % per == 0 and c not in (0, CHUNKS - 1):
-                for copy in copies(c):
-                    copy.wait()
+            c = tile * TALL // per
+            if tile * TALL % per == 0:
+                if 0 < c < CHUNKS - 1:
+                    for copy in copies(c):
+                        copy.wait()
+                if c + AHEAD < CHUNKS - 1:
+                    for copy in copies(c + AHEAD):
+                        copy.start()
         else:
-            c = lax.div(tile, per // 8)
-
-            @pl.when((lax.rem(tile, per // 8) == 0) & (c > 0) & (c < CHUNKS - 1))
+            c = lax.div(tile, per // TALL)
+            first = lax.rem(tile, per // TALL) == 0
+
+            @pl.when(first & (c > 0) & (c < CHUNKS - 1))
             def _():
                 for copy in copies(c):
                     copy.wait()
 
+            @pl.when(first & (c < CHUNKS - 1 - AHEAD))
+            def _():
+                for copy in copies(c + AHEAD):
+                    copy.start()
+
     def prepare(tile, carry):
-        row = tile * 8 if isinstance(tile, int) else pl.multiple_of(tile * 8, 8)
+        row = tile * TALL if isinstance(tile, int) else pl.multiple_of(tile * TALL, 8)
         at = row + 8
         for b in range(nblk):
-            fields = prologue(row, b)
+            fields = prologue(row, b, TALL)
             for f in (A, B, T):
-                s0[f - A, b, pl.ds(at, 8), :] = fields[f]
+                s0[f - A, b, pl.ds(at, TALL), :] = fields[f]
             for f in range(PR, FIELDS):
-                coef[f - PR, b, pl.ds(at, 8), :] = fields[f]
+                coef[f - PR, b, pl.ds(at, TALL), :] = fields[f]
             if b == 0:
-                packed[0, pl.ds(row, 8), :] = pack(fields, 0)
+                packed[0, pl.ds(row, TALL), :] = pack(fields, 0)
             if b == nblk - 1:
-                packed[1, pl.ds(row, 8), :] = pack(fields, 8)
+                packed[1, pl.ds(row, TALL), :] = pack(fields, 8)
         return carry
 
     def at_row(tile):
-        return tile * 8 + 8 if isinstance(tile, int) else pl.multiple_of(tile * 8 + 8, 8)
+        return tile * TALL + 8 if isinstance(tile, int) else pl.multiple_of(tile * TALL + 8, 8)
 
     def stress_at(level):
         def phase(tile, carry):
@@ -336,7 +350,7 @@
 
     def put_stress(tile, blocks):
         na, nb, nt = blocks
-        r = pl.ds(tile * 8, 8) if isinstance(tile, int) else pl.ds(pl.multiple_of(tile * 8, 8), 8)
+        r = pl.ds(at_row(tile) - 8, TALL)
         for b in range(nblk):
             l = slice(b * LANES, (b + 1) * LANES)
             out_str[0, r, l] = 0.5 * (na[b] + nb[b])
@@ -347,23 +361,23 @@
         put_stress(tile, stress_phase(main, ITERS - 1, at_row(tile)))
         return carry
 
-    inner = [None] * nblk
-    inner[0] = lane >= 4
-    inner[nblk - 1] = lane < LANES - 4
+    tall_inner = [None] * nblk
+    tall_inner[0] = tall_lane >= 4
+    tall_inner[nblk - 1] = tall_lane < LANES - 4
 
     def last_velocity(tile, carry):
         u, v, nu, nv, inert = velocity_phase(main, ITERS - 1, at_row(tile))
-        r = pl.ds(tile * 8, 8) if isinstance(tile, int) else pl.ds(pl.multiple_of(tile * 8, 8), 8)
+        r = pl.ds(at_row(tile) - 8, TALL)
         for b in range(nblk):
             l = slice(b * LANES, (b + 1) * LANES)
             out_vel[0, r, l] = nu[b]
             out_vel[1, r, l] = nv[b]
-        res, kin = square_sums((u, v, nu, nv, inert), inner)
-        keep = jnp.int32(0) + row_ids() + tile * 8
+        res, kin = square_sums((u, v, nu, nv, inert), tall_inner)
+        keep = row_ids(TALL) + tile * TALL
         good = (keep >= 4) & (keep < nrow - 4)
         return carry[0] + jnp.where(good, res, 0.0), carry[1] + jnp.where(good, kin, 0.0)
 
-    zero = jnp.zeros((8, LANES), F32)
+    zero = jnp.zeros((TALL, LANES), F32)
     wavefront(
         tiles,
         [(0, prepare), (1, stress_at(0)), (3, velocity_at(0)), (4, stress_at(1)), (6, velocity_at(1))],
@@ -375,7 +389,7 @@
         copy.wait()
     no_outside(rows0, gx, ngx)
     for side, b, shift in ((0, 0, 0), (1, nblk - 1, 8)):
-        for at, to in ((BOT_HALO, nrow), (TOP_HALO, nrow + LANES - 8)):
+        for at, to in ((BOT_HALO, nrow), (TOP_HALO - 4, nrow + LANES - 8)):
             packed[side, pl.ds(to, 8), :] = pack([rows0[f, b, pl.ds(at, 8), :] for f in range(FIELDS)], shift)
         for blk in range(row_blks + 1):
             flat = packed[side, pl.ds(blk * LANES, LANES), :].T
@@ -401,24 +415,28 @@
         return get
 
     def sweep_strip(dom):
-        own = {}
+        ends = {}
         for level in range(ITERS):
-            for at in (TOP_HALO, TOP_OWN, BOT_OWN, BOT_HALO):
+            for at in (8, 16, 24):
                 stress_phase(dom, level, at)
-            for at in (TOP_HALO, TOP_OWN, BOT_OWN, BOT_HALO):
-                own[at] = velocity_phase(dom, level, at)
-        return own
+            for at in (8, 16, 24) if level < ITERS - 1 else (8, 24):
+                ends[at] = velocity_phase(dom, level, at)
+        return ends
 
     def add(sums, more):
         return sums[0] + more[0], sums[1] + more[1]
 
     sub = row_ids()
+    sums = [sum(x[8 * i : 8 * i + 8] for i in range(TALL // 8)) for x in sums]
+    inner = [None] * nblk
+    inner[0] = lane >= 4
+    inner[nblk - 1] = lane < LANES - 4
     row_dom = Domain(nblk, strip_get(rows0, rows_uv, rows_s))
-    own = sweep_strip(row_dom)
+    ends = sweep_strip(row_dom)
+    for at, good in ((8, sub >= 4), (24, sub < 4)):
+        sums = add(sums, square_sums(ends[at], [good if m is None else good & m for m in inner]))
     for at, row, good in ((TOP_OWN, 0, sub < 4), (BOT_OWN, nrow - 8, sub >= 4)):
-        keep = [good if m is None else good & m for m in inner]
-        sums = add(sums, square_sums(own[at], keep))
-        _, _, nu, nv, _ = own[at]
+        nu, nv = (row_dom.read(f, ITERS, at) for f in (U, V))
         sa, sb, st = (row_dom.read(f, ITERS, at) for f in (A, B, T))
         for b in range(nblk):
             r, l = pl.ds(row, 8), slice(b * LANES, (b + 1) * LANES)
@@ -432,10 +450,30 @@
         copy.wait()
     no_outside(cols0, gy, ngy)
     col_dom = Domain(row_blks + 1, strip_get(cols0, cols_uv, cols_s))
-    own = sweep_strip(col_dom)
-    for side, (at, good) in enumerate(((TOP_OWN, sub < 4), (BOT_OWN, sub >= 4))):
-        sums = add(sums, square_sums(own[at], [good] * row_blks + [False]))
-        _, _, nu, nv, _ = own[at]
+    ends = sweep_strip(col_dom)
+    for at, good in ((8, sub >= 4), (24, sub < 4)):
+        sums = add(sums, square_sums(ends[at], [good] * row_blks + [False]))
+
+    half = LANES // 2
+    both = [x + pltpu.roll(x, half, 1) for x in sums]
+    mine = jnp.where(lane < half, both[0], both[1])
+    gather_x[gx, 0:1, :] = jnp.sum(mine, axis=0, keepdims=True)
+
+    def spread(axis, slots, me, count):
+        return [
+            pltpu.make_async_remote_copy(
+                src_ref=slots.at[me, pl.ds(0, 1), :],
+                dst_ref=slots.at[me, pl.ds(0, 1), :],
+                send_sem=sum_send.at[axis, d],
+                recv_sem=sum_recv.at[axis, d],
+                device_id=peer(axis, d),
+                device_id_type=pl.DeviceIdType.MESH,
+            )
+            for d in range(1, count)
+        ]
+
+    for side, at in enumerate((TOP_OWN, BOT_OWN)):
+        nu, nv = (col_dom.read(f, ITERS, at) for f in (U, V))
         sa, sb, st = (col_dom.read(f, ITERS, at) for f in (A, B, T))
         for blk in range(row_blks):
             values = (
@@ -444,6 +482,9 @@
             )
             for i, x in enumerate(values):
                 turned[blk, pl.ds(40 * side + 8 * i, 8), :] = x
+    x_copies = spread(0, gather_x, gx, ngx)
+    for copy in x_copies:
+        copy.start()
     for blk in range(row_blks):
         packed[0, pl.ds(blk * LANES, LANES), :] = turned[blk].T
 
@@ -465,9 +506,21 @@
             ref[at, r, l] = value
         return carry
 
-    lax.fori_loop(0, tiles, merge, 0, unroll=4)
-    out_sum[0] = sums[0]
-    out_sum[1] = sums[1]
+    lax.fori_loop(0, nrow // 16, merge, 0, unroll=4)
+    for copy in x_copies:
+        copy.wait()
+    gather_y[gy, 0:1, :] = sum(gather_x[i, 0:1, :] for i in range(ngx))
+    y_copies = spread(1, gather_y, gy, ngy)
+    for copy in y_copies:
+        copy.start()
+    lax.fori_loop(nrow // 16, nrow // 8, merge, 0, unroll=4)
+    for copy in y_copies:
+        copy.wait()
+    total = sum(gather_y[i, 0:1, :] for i in range(ngy))
+    cells = nrow * ngx * ncol * ngy
+    low = lax.broadcasted_iota(jnp.int32, (1, LANES), 1) < half
+    out_res[0, 0] = jnp.sum(jnp.where(low, total, 0.0)) * (1.0 / cells)
+    out_kin[0, 0] = jnp.sum(jnp.where(low, 0.0, total)) * (0.5 * time_step / 4.0 / cells)
 
 
 def per_device(velocity, stress, strength, ice_mass, wind_stress, current, ice_mask, open_water):
@@ -478,15 +531,18 @@
     vmem = pltpu.VMEM
     any_spec = pl.BlockSpec(memory_space=pl.ANY)
     vmem_spec = pl.BlockSpec(memory_space=pltpu.VMEM)
-    new_velocity, new_stress, parts = pl.pallas_call(
+    smem_spec = pl.BlockSpec(memory_space=pltpu.SMEM)
+    ngx, ngy = lax.axis_size(GX), lax.axis_size(GY)
+    new_velocity, new_stress, residual, kinetic = pl.pallas_call(
         main_kernel,
         out_shape=(
-            jax.ShapeDtypeStruct(velocity.shape, F32),
-            jax.ShapeDtypeStruct(stress.shape, F32),
-            jax.ShapeDtypeStruct((2, 8, LANES), F32),
+            vmem(velocity.shape, F32),
+            vmem(stress.shape, F32),
+            jax.ShapeDtypeStruct((1, 1), F32),
+            jax.ShapeDtypeStruct((1, 1), F32),
         ),
         in_specs=[any_spec] * 8,
-        out_specs=(vmem_spec, vmem_spec, vmem_spec),
+        out_specs=(vmem_spec, vmem_spec, smem_spec, smem_spec),
         scratch_shapes=[
             vmem((2, nblk, pad, LANES), F32),
             vmem((3, nrow, ncol), F32),
@@ -509,23 +565,20 @@
             vmem((ITERS, 2, row_blks + 1, STRIP_ROWS, LANES), F32),
             vmem((ITERS, 3, row_blks + 1, STRIP_ROWS, LANES), F32),
             vmem((row_blks, LANES, LANES), F32),
+            vmem((ngx, 8, LANES), F32),
+            vmem((ngy, 8, LANES), F32),
             pltpu.SemaphoreType.DMA((nblk + 7, CHUNKS)),
             pltpu.SemaphoreType.DMA((2, 2)),
             pltpu.SemaphoreType.DMA((2, 2)),
+            pltpu.SemaphoreType.DMA((2, max(ngx, ngy))),
+            pltpu.SemaphoreType.DMA((2, max(ngx, ngy))),
         ],
         compiler_params=pltpu.CompilerParams(
-            collective_id=0, has_side_effects=True, vmem_limit_bytes=62 * 1024 * 1024
+            collective_id=0, has_side_effects=True, vmem_limit_bytes=57 * 1024 * 1024
         ),
         name="subcycles",
     )(velocity, stress, strength, ice_mass, wind_stress, current, ice_mask, open_water)
-    totals = lax.psum(jnp.sum(parts, axis=(1, 2)), AXES)
-    cells = nrow * lax.axis_size(GX) * ncol * lax.axis_size(GY)
-    return (
-        new_velocity,
-        new_stress,
-        totals[0] / cells,
-        totals[1] * (0.5 * time_step / 4.0) / cells,
-    )
+    return new_velocity, new_stress, residual.reshape(()), kinetic.reshape(())
 
 
 def solution(mesh):

time: 109 us -> 44.9 us (0.41)
  blocking collectives: 66.2 us -> 0 us
  Pallas kernels: 31.9 us -> 37.7 us
  local copies, waits for them, and re-layouts: 5.49 us -> 2.99 us
    psum x1 -> x0, blocking collectives: 66.2 us -> none  [per_device(): totals = lax.psum(jnp.sum(parts, axis=(1, 2)), AXES)]
    pallas_call x1, Pallas kernels: 31.9 us -> 37.7 us  [per_device(): pl.pallas_call(main_kernel, out_shape=(vmem(velocity.shape, F32), vmem(st...]
    unnamed x4 -> x2, local copies, waits for them, and re-layouts: 4.91 us -> 2.99 us
where the time goes in v1:
time: 44.9 us; the launch traced here: 44.7 us
  Pallas kernels  37.7 us (84%)
  between operations  4.09 us (9%)
  local copies, waits for them, and re-layouts  2.99 us (7%)
    pallas_call x1, Pallas kernels, per_device(): pl.pallas_call(main_kernel, out_shape=(vmem(velocity.shape, F32), vmem(st...  37.7 us
    unnamed x2, local copies, waits for them, and re-layouts  2.99 us

profile of v1, /device:TPU:1, one launch (start us, length us, event | category | flops | bytes accessed | tf_op | source)
XLA Modules:
  0.0 44.7 jit_solution(17986794096622674226)
XLA Ops:
  0.6 37.7 %subcycles.1 = (f32[2,512,512]{2,1,0:T(8,128)S(1)}, f32[3,512,512]{2,1,0:T(8,128)S(1)}, f32[1,1]{1,0:T(1,128)}, f32[1,1]{1,0:T(1,128)}) custom-call(f32[2,512,512]{2,1,0:T(8,128)} %vel.1, f32[3,512,512]{2,1,0:T(8,128)} %stress.1, f32[512,512]{1,0:T(8,128)} %strength.1, f32[512,512]{1,0:T(8,128)} %mass.1, f32[2,512,512]{2,1,0:T(8,128)} %wind.1, ...), custom_call_target="tpu_custom_call" | custom-call | tf_op jit(solution)/shard_map/subcycles/pallas_call | solution.py:536
  38.3 1.3 %copy.16 = f32[2,512,512]{2,1,0:T(8,128)} copy(f32[2,512,512]{2,1,0:T(8,128)S(1)} %get-tuple-element.12) | data formatting | bytes 4194304
  39.6 1.7 %copy.17 = f32[3,512,512]{2,1,0:T(8,128)} copy(f32[3,512,512]{2,1,0:T(8,128)S(1)} %get-tuple-element.13) | data formatting | bytes 6291456

commit v2 on v1

--- a/solution.py
+++ b/solution.py
@@ -24,10 +24,12 @@
 LANES = 128
 CHUNKS = 8
 AHEAD = 3
+MIDWAY = 3
 TALL = 16
 FIELDS = 11
 U, V, A, B, T, PR, AL, BE, IN, KU, KV = range(FIELDS)
 SWAPPED = (V, U, B, A, T, PR, AL, BE, IN, KV, KU)
+SPLIT = 6
 STRIP_ROWS = 40
 TOP_HALO, TOP_OWN, BOT_OWN, BOT_HALO = 8, 12, 20, 28
 
@@ -149,19 +151,35 @@
     return res, kin
 
 
-def wavefront(tiles, phases, carry, arrive=None):
+def wavefront(tiles, phases, carry, arrive=None, group=1, midway=None):
     depth = max(lag for lag, _ in phases)
 
     def step(t, carry, active):
-        if arrive is not None and active[0][0] == 0:
-            arrive(t)
-        for lag, phase in reversed(active):
+        for lag, phase in active:
             carry = phase(t - lag, carry)
         return carry
 
+    def steady(t, carry):
+        return step(t, carry, phases)
+
     for t in range(depth):
+        if arrive is not None and t % group == 0:
+            arrive(t // group)
         carry = step(t, carry, [p for p in phases if p[0] <= t])
-    carry = lax.fori_loop(depth, tiles, lambda t, c: step(t, c, phases), carry)
+    if arrive is None:
+        carry = lax.fori_loop(depth, tiles, steady, carry)
+    else:
+        whole = -(-depth // group)
+        if depth < whole * group:
+            carry = lax.fori_loop(depth, whole * group, steady, carry)
+
+        def run_group(c, carry):
+            arrive(c)
+            return lax.fori_loop(c * group, (c + 1) * group, steady, carry)
+
+        carry = lax.fori_loop(whole, MIDWAY, run_group, carry)
+        midway()
+        carry = lax.fori_loop(MIDWAY, tiles // group, run_group, carry)
     for t in range(tiles, tiles + depth):
         carry = step(t, carry, [p for p in phases if t - p[0] < tiles])
     return carry
@@ -194,7 +212,7 @@
             out.append((src.at[r, :], dst.at[r, :]))
         return [pltpu.make_async_copy(s, d, in_sem.at[i, c]) for i, (s, d) in enumerate(out)]
 
-    for c in [0, CHUNKS - 1] + list(range(1, AHEAD)):
+    for c in list(range(AHEAD)) + [CHUNKS - 1]:
         for copy in copies(c):
             copy.start()
 
@@ -233,14 +251,6 @@
             4.0 * (wind_in[1, r, l] + drag_coef * cur_in[1, r, l]),
         ]
 
-    for c in (0, CHUNKS - 1):
-        for copy in copies(c):
-            copy.wait()
-    for row, at in ((0, TOP_OWN), (nrow - 8, BOT_OWN)):
-        for b in range(nblk):
-            for f, x in enumerate(prologue(row, b, 8)):
-                rows0[f, b, pl.ds(at, 8), :] = x
-
     def exchange(strip, axis):
         out = []
         for way, (step, src, dst) in enumerate(((-1, TOP_OWN, BOT_HALO), (1, BOT_OWN + 4, TOP_HALO))):
@@ -265,10 +275,18 @@
         def _():
             strip[:, :, BOT_HALO : BOT_HALO + 4, :] = jnp.zeros(strip.shape[:2] + (4, LANES), F32)
 
-    pl.semaphore_wait(barrier, ngx + ngy - 2)
     row_copies = exchange(rows0, 0)
-    for copy in row_copies:
-        copy.start()
+
+    def send_rows():
+        for copy in copies(CHUNKS - 1):
+            copy.wait()
+        for row, at in ((0, TOP_OWN), (nrow - 8, BOT_OWN)):
+            for b in range(nblk):
+                for f, x in enumerate(prologue(row, b, 8)):
+                    rows0[f, b, pl.ds(at, 8), :] = x
+        pl.semaphore_wait(barrier, ngx + ngy - 2)
+        for copy in row_copies:
+            copy.start()
 
     uvs, ss = (uv0, uv1, uv2, uv3, uv4), (s0, s1, s2, s3, s4)
 
@@ -283,35 +301,33 @@
     lane = lane_ids()
     tall_lane = lane_ids(TALL)
 
-    def pack(tile_fields, shift):
-        out = None
-        for slot, f in enumerate(SWAPPED):
-            x = tile_fields[f]
-            by = (8 * slot + shift) % LANES
-            x = pltpu.roll(x, by, 1) if by else x
-            out = x if out is None else jnp.where(lane_ids(x.shape[0]) < 8 * slot, out, x)
+    def pack(first, last):
+        lanes = lane_ids(first[0].shape[0])
+        out = []
+        for names in (SWAPPED[:SPLIT], SWAPPED[SPLIT:]):
+            edges = [jnp.where(lanes < LANES // 2, first[f], last[f]) for f in names]
+            total = pltpu.roll(edges[1], 16, 1)
+            for q in range(2, len(edges)):
+                total = jnp.where(lanes < 16 * q - 8, total, pltpu.roll(edges[q], 16 * q, 1))
+            out.append(jnp.where((lanes < 8) | (lanes >= LANES - 8), edges[0], total))
         return out
 
-    def arrive(tile):
-        if isinstance(tile, int):
-            c = tile * TALL // per
-            if tile * TALL % per == 0:
-                if 0 < c < CHUNKS - 1:
-                    for copy in copies(c):
-                        copy.wait()
-                if c + AHEAD < CHUNKS - 1:
-                    for copy in copies(c + AHEAD):
-                        copy.start()
+    def arrive(c):
+        if isinstance(c, int):
+            if c < CHUNKS - 1:
+                for copy in copies(c):
+                    copy.wait()
+            if c + AHEAD < CHUNKS - 1:
+                for copy in copies(c + AHEAD):
+                    copy.start()
         else:
-            c = lax.div(tile, per // TALL)
-            first = lax.rem(tile, per // TALL) == 0
-
-            @pl.when(first & (c > 0) & (c < CHUNKS - 1))
+
+            @pl.when(c < CHUNKS - 1)
             def _():
                 for copy in copies(c):
                     copy.wait()
 
-            @pl.when(first & (c < CHUNKS - 1 - AHEAD))
+            @pl.when(c < CHUNKS - 1 - AHEAD)
             def _():
                 for copy in copies(c + AHEAD):
                     copy.start()
@@ -319,16 +335,17 @@
     def prepare(tile, carry):
         row = tile * TALL if isinstance(tile, int) else pl.multiple_of(tile * TALL, 8)
         at = row + 8
+        edges = []
         for b in range(nblk):
             fields = prologue(row, b, TALL)
             for f in (A, B, T):
                 s0[f - A, b, pl.ds(at, TALL), :] = fields[f]
             for f in range(PR, FIELDS):
                 coef[f - PR, b, pl.ds(at, TALL), :] = fields[f]
-            if b == 0:
-                packed[0, pl.ds(row, TALL), :] = pack(fields, 0)
-            if b == nblk - 1:
-                packed[1, pl.ds(row, TALL), :] = pack(fields, 8)
+            if b in (0, nblk - 1):
+                edges.append(fields)
+        for i, x in enumerate(pack(edges[0], edges[-1])):
+            packed[i, pl.ds(row, TALL), :] = x
         return carry
 
     def at_row(tile):
@@ -380,29 +397,34 @@
     zero = jnp.zeros((TALL, LANES), F32)
     wavefront(
         tiles,
-        [(0, prepare), (1, stress_at(0)), (3, velocity_at(0)), (4, stress_at(1)), (6, velocity_at(1))],
+        [(6, velocity_at(1)), (4, stress_at(1)), (3, velocity_at(0)), (1, stress_at(0)), (0, prepare)],
         0,
         arrive,
+        per // TALL,
+        send_rows,
     )
 
     for copy in row_copies:
         copy.wait()
     no_outside(rows0, gx, ngx)
-    for side, b, shift in ((0, 0, 0), (1, nblk - 1, 8)):
-        for at, to in ((BOT_HALO, nrow), (TOP_HALO - 4, nrow + LANES - 8)):
-            packed[side, pl.ds(to, 8), :] = pack([rows0[f, b, pl.ds(at, 8), :] for f in range(FIELDS)], shift)
+    for at, to in ((BOT_HALO, nrow), (TOP_HALO - 4, nrow + LANES - 8)):
+        ends = [[rows0[f, b, pl.ds(at, 8), :] for f in range(FIELDS)] for b in (0, nblk - 1)]
+        for i, x in enumerate(pack(*ends)):
+            packed[i, pl.ds(to, 8), :] = x
+    for i, names in enumerate((range(SPLIT), range(SPLIT, FIELDS))):
         for blk in range(row_blks + 1):
-            flat = packed[side, pl.ds(blk * LANES, LANES), :].T
-            for f in range(FIELDS):
-                x = flat[8 * f : 8 * f + 8, :]
-                cols0[f, blk, pl.ds((TOP_OWN, BOT_OWN)[side], 8), :] = -x if f == BE else x
+            flat = packed[i, pl.ds(blk * LANES, LANES), :].T
+            for q, f in enumerate(names):
+                for at, to in ((16 * q, TOP_OWN), ((16 * q - 8) % LANES, BOT_OWN)):
+                    x = flat[at : at + 8, :]
+                    cols0[f, blk, pl.ds(to, 8), :] = -x if f == BE else x
     col_copies = exchange(cols0, 1)
     for copy in col_copies:
         copy.start()
 
     sums = wavefront(
         tiles,
-        [(0, stress_at(2)), (2, velocity_at(2)), (3, last_stress), (5, last_velocity)],
+        [(5, last_velocity), (3, last_stress), (2, velocity_at(2)), (0, stress_at(2))],
         (zero, zero),
     )
 
@@ -414,14 +436,19 @@
 
         return get
 
-    def sweep_strip(dom):
-        ends = {}
-        for level in range(ITERS):
-            for at in (8, 16, 24):
-                stress_phase(dom, level, at)
-            for at in (8, 16, 24) if level < ITERS - 1 else (8, 24):
-                ends[at] = velocity_phase(dom, level, at)
-        return ends
+    for copy in col_copies:
+        copy.wait()
+    no_outside(cols0, gy, ngy)
+    row_dom = Domain(nblk, strip_get(rows0, rows_uv, rows_s))
+    col_dom = Domain(row_blks + 1, strip_get(cols0, cols_uv, cols_s))
+    row_ends, col_ends = {}, {}
+    for level in range(ITERS):
+        for at in (8, 16, 24):
+            stress_phase(row_dom, level, at)
+            stress_phase(col_dom, level, at)
+        for at in (8, 16, 24) if level < ITERS - 1 else (8, 24):
+            row_ends[at] = velocity_phase(row_dom, level, at)
+            col_ends[at] = velocity_phase(col_dom, level, at)
 
     def add(sums, more):
         return sums[0] + more[0], sums[1] + more[1]
@@ -431,28 +458,9 @@
     inner = [None] * nblk
     inner[0] = lane >= 4
     inner[nblk - 1] = lane < LANES - 4
-    row_dom = Domain(nblk, strip_get(rows0, rows_uv, rows_s))
-    ends = sweep_strip(row_dom)
     for at, good in ((8, sub >= 4), (24, sub < 4)):
-        sums = add(sums, square_sums(ends[at], [good if m is None else good & m for m in inner]))
-    for at, row, good in ((TOP_OWN, 0, sub < 4), (BOT_OWN, nrow - 8, sub >= 4)):
-        nu, nv = (row_dom.read(f, ITERS, at) for f in (U, V))
-        sa, sb, st = (row_dom.read(f, ITERS, at) for f in (A, B, T))
-        for b in range(nblk):
-            r, l = pl.ds(row, 8), slice(b * LANES, (b + 1) * LANES)
-            for ref, i, x in (
-                (out_vel, 0, nu[b]), (out_vel, 1, nv[b]),
-                (out_str, 0, 0.5 * (sa[b] + sb[b])), (out_str, 1, 0.5 * (sa[b] - sb[b])), (out_str, 2, 0.5 * st[b]),
-            ):
-                ref[i, r, l] = jnp.where(good, x, ref[i, r, l])
-
-    for copy in col_copies:
-        copy.wait()
-    no_outside(cols0, gy, ngy)
-    col_dom = Domain(row_blks + 1, strip_get(cols0, cols_uv, cols_s))
-    ends = sweep_strip(col_dom)
-    for at, good in ((8, sub >= 4), (24, sub < 4)):
-        sums = add(sums, square_sums(ends[at], [good] * row_blks + [False]))
+        sums = add(sums, square_sums(row_ends[at], [good if m is None else good & m for m in inner]))
+        sums = add(sums, square_sums(col_ends[at], [good] * row_blks + [False]))
 
     half = LANES // 2
     both = [x + pltpu.roll(x, half, 1) for x in sums]
@@ -472,7 +480,8 @@
             for d in range(1, count)
         ]
 
-    for side, at in enumerate((TOP_OWN, BOT_OWN)):
+    x_copies = spread(0, gather_x, gx, ngx)
+    for back, at in ((0, TOP_OWN), (8, BOT_OWN)):
         nu, nv = (col_dom.read(f, ITERS, at) for f in (U, V))
         sa, sb, st = (col_dom.read(f, ITERS, at) for f in (A, B, T))
         for blk in range(row_blks):
@@ -481,12 +490,21 @@
                 0.5 * (sb[blk] + sa[blk]), 0.5 * (sb[blk] - sa[blk]), 0.5 * st[blk],
             )
             for i, x in enumerate(values):
-                turned[blk, pl.ds(40 * side + 8 * i, 8), :] = x
-    x_copies = spread(0, gather_x, gx, ngx)
+                turned[blk, pl.ds((16 * i - back) % LANES, 8), :] = x
     for copy in x_copies:
         copy.start()
     for blk in range(row_blks):
         packed[0, pl.ds(blk * LANES, LANES), :] = turned[blk].T
+    for at, row, good in ((TOP_OWN, 0, sub < 4), (BOT_OWN, nrow - 8, sub >= 4)):
+        nu, nv = (row_dom.read(f, ITERS, at) for f in (U, V))
+        sa, sb, st = (row_dom.read(f, ITERS, at) for f in (A, B, T))
+        for b in range(nblk):
+            r, l = pl.ds(row, 8), slice(b * LANES, (b + 1) * LANES)
+            for ref, i, x in (
+                (out_vel, 0, nu[b]), (out_vel, 1, nv[b]),
+                (out_str, 0, 0.5 * (sa[b] + sb[b])), (out_str, 1, 0.5 * (sa[b] - sb[b])), (out_str, 2, 0.5 * st[b]),
+            ):
+                ref[i, r, l] = jnp.where(good, x, ref[i, r, l])
 
     def merge(tile, carry):
         r = pl.ds(pl.multiple_of(tile * 8, 8), 8)
@@ -495,13 +513,9 @@
         first, last = slice(0, LANES), slice(ncol - LANES, ncol)
         new = []
         for i, (ref, at) in enumerate(places):
-            left = pltpu.roll(x, (LANES - 8 * i) % LANES, 1) if i else x
-            right = pltpu.roll(x, (LANES - 8 - 40 - 8 * i) % LANES, 1)
-            if first == last:
-                new.append((ref, at, first, jnp.where(lane < 4, left, jnp.where(lane >= LANES - 4, right, ref[at, r, first]))))
-            else:
-                new.append((ref, at, first, jnp.where(lane < 4, left, ref[at, r, first])))
-                new.append((ref, at, last, jnp.where(lane >= LANES - 4, right, ref[at, r, last])))
+            edge = pltpu.roll(x, LANES - 16 * i, 1) if i else x
+            new.append((ref, at, first, jnp.where(lane < 4, edge, ref[at, r, first])))
+            new.append((ref, at, last, jnp.where(lane >= LANES - 4, edge, ref[at, r, last])))
         for ref, at, l, value in new:
             ref[at, r, l] = value
         return carry
@@ -521,6 +535,17 @@
     low = lax.broadcasted_iota(jnp.int32, (1, LANES), 1) < half
     out_res[0, 0] = jnp.sum(jnp.where(low, total, 0.0)) * (1.0 / cells)
     out_kin[0, 0] = jnp.sum(jnp.where(low, 0.0, total)) * (0.5 * time_step / 4.0 / cells)
+
+
+def store_kernel(vel, stress, residual, kinetic, out_vel, out_str, out_res, out_kin, sem):
+    copies = [pltpu.make_async_copy(vel.at[i], out_vel.at[i], sem.at[i]) for i in range(2)]
+    copies += [pltpu.make_async_copy(stress.at[i], out_str.at[i], sem.at[2 + i]) for i in range(3)]
+    for copy in copies:
+        copy.start()
+    out_res[0, 0] = residual[0, 0]
+    out_kin[0, 0] = kinetic[0, 0]
+    for copy in copies:
+        copy.wait()
 
 
 def per_device(velocity, stress, strength, ice_mass, wind_stress, current, ice_mask, open_water):
@@ -578,6 +603,20 @@
         ),
         name="subcycles",
     )(velocity, stress, strength, ice_mass, wind_stress, current, ice_mask, open_water)
+    new_velocity, new_stress, residual, kinetic = pl.pallas_call(
+        store_kernel,
+        out_shape=(
+            jax.ShapeDtypeStruct(velocity.shape, F32),
+            jax.ShapeDtypeStruct(stress.shape, F32),
+            jax.ShapeDtypeStruct((1, 1), F32),
+            jax.ShapeDtypeStruct((1, 1), F32),
+        ),
+        in_specs=[vmem_spec, vmem_spec, smem_spec, smem_spec],
+        out_specs=(any_spec, any_spec, smem_spec, smem_spec),
+        scratch_shapes=[pltpu.SemaphoreType.DMA((5,))],
+        compiler_params=pltpu.CompilerParams(vmem_limit_bytes=1024 * 1024),
+        name="store",
+    )(new_velocity, new_stress, residual, kinetic)
     return new_velocity, new_stress, residual.reshape(()), kinetic.reshape(())
 
 

time: 44.9 us -> 40.4 us (0.90)
  between operations: 4.09 us -> 0.64 us
  local copies, waits for them, and re-layouts: 2.99 us -> 0 us
  Pallas kernels: 37.7 us -> 39.6 us
    pallas_call x0 -> x1, Pallas kernels: none -> 4.18 us  [per_device(): pl.pallas_call(store_kernel, out_shape=(jax.ShapeDtypeStruct(velocity.sha...]
    unnamed x2 -> x0, local copies, waits for them, and re-layouts: 2.99 us -> none
    pallas_call x1, Pallas kernels: 37.7 us -> 35.4 us  [per_device(): pl.pallas_call(main_kernel, out_shape=(vmem(velocity.shape, F32), vmem(st...]
where the time goes in v2:
time: 40.4 us; the launch traced here: 40.2 us
  Pallas kernels  39.6 us (98%)
  between operations  0.64 us (2%)
    pallas_call x1, Pallas kernels, per_device(): pl.pallas_call(main_kernel, out_shape=(vmem(velocity.shape, F32), vmem(st...  35.4 us
    pallas_call x1, Pallas kernels, per_device(): pl.pallas_call(store_kernel, out_shape=(jax.ShapeDtypeStruct(velocity.sha...  4.18 us

profile of v2, /device:TPU:1, one launch (start us, length us, event | category | flops | bytes accessed | tf_op | source)
XLA Modules:
  0.0 40.2 jit_solution(17079277585862059966)
XLA Ops:
  0.6 35.4 %subcycles.1 = (f32[2,512,512]{2,1,0:T(8,128)S(1)}, f32[3,512,512]{2,1,0:T(8,128)S(1)}, f32[1,1]{1,0:T(1,128)}, f32[1,1]{1,0:T(1,128)}) custom-call(f32[2,512,512]{2,1,0:T(8,128)} %vel.1, f32[3,512,512]{2,1,0:T(8,128)} %stress.1, f32[512,512]{1,0:T(8,128)} %strength.1, f32[512,512]{1,0:T(8,128)} %mass.1, f32[2,512,512]{2,1,0:T(8,128)} %wind.1, ...), custom_call_target="tpu_custom_call" | custom-call | tf_op jit(solution)/shard_map/subcycles/pallas_call | solution.py:561
  36.1 4.2 %store.1 = (f32[2,512,512]{2,1,0:T(8,128)}, f32[3,512,512]{2,1,0:T(8,128)}, f32[1,1]{1,0:T(1,128)}, f32[1,1]{1,0:T(1,128)}) custom-call(f32[2,512,512]{2,1,0:T(8,128)S(1)} %get-tuple-element.12.vel, f32[3,512,512]{2,1,0:T(8,128)S(1)} %get-tuple-element.13.stress, f32[1,1]{1,0:T(1,128)} %get-tuple-element.14.residual, f32[1,1]{1,0:T(1,128)} %get-tuple-element.15.kinetic), custom_call_target="tpu_custom_call" | custom-call | tf_op jit(solution)/shard_map/store/pallas_call | solution.py:606

commit v3 on v2

--- a/solution.py
+++ b/solution.py
@@ -177,9 +177,10 @@
             arrive(c)
             return lax.fori_loop(c * group, (c + 1) * group, steady, carry)
 
-        carry = lax.fori_loop(whole, MIDWAY, run_group, carry)
+        middle = max(whole, MIDWAY)
+        carry = lax.fori_loop(whole, middle, run_group, carry)
         midway()
-        carry = lax.fori_loop(MIDWAY, tiles // group, run_group, carry)
+        carry = lax.fori_loop(middle, tiles // group, run_group, carry)
     for t in range(tiles, tiles + depth):
         carry = step(t, carry, [p for p in phases if t - p[0] < tiles])
     return carry
@@ -187,7 +188,7 @@
 
 def main_kernel(
     vel, stress, strength, mass, wind, current, mask, water,
-    out_vel, out_str, out_res, out_kin,
+    out_vel, out_str, out_sum,
     uv0, str_in, strength_in, mass_in, wind_in, cur_in, mask_in, water_in,
     uv1, uv2, uv3, uv4, s0, s1, s2, s3, s4, coef,
     packed, rows0, rows_uv, rows_s, cols0, cols_uv, cols_s, turned,
@@ -210,7 +211,8 @@
             out.append((src.at[:, r, :], dst.at[:, r, :]))
         for src, dst in ((strength, strength_in), (mass, mass_in), (mask, mask_in), (water, water_in)):
             out.append((src.at[r, :], dst.at[r, :]))
-        return [pltpu.make_async_copy(s, d, in_sem.at[i, c]) for i, (s, d) in enumerate(out)]
+        slot = AHEAD if isinstance(c, int) and c == CHUNKS - 1 else lax.rem(c, AHEAD)
+        return [pltpu.make_async_copy(s, d, in_sem.at[i, slot]) for i, (s, d) in enumerate(out)]
 
     for c in list(range(AHEAD)) + [CHUNKS - 1]:
         for copy in copies(c):
@@ -397,7 +399,7 @@
     zero = jnp.zeros((TALL, LANES), F32)
     wavefront(
         tiles,
-        [(6, velocity_at(1)), (4, stress_at(1)), (3, velocity_at(0)), (1, stress_at(0)), (0, prepare)],
+        [(8, velocity_at(1)), (6, stress_at(1)), (4, velocity_at(0)), (2, stress_at(0)), (0, prepare)],
         0,
         arrive,
         per // TALL,
@@ -424,7 +426,7 @@
 
     sums = wavefront(
         tiles,
-        [(5, last_velocity), (3, last_stress), (2, velocity_at(2)), (0, stress_at(2))],
+        [(6, last_velocity), (4, last_stress), (2, velocity_at(2)), (0, stress_at(2))],
         (zero, zero),
     )
 
@@ -472,8 +474,8 @@
             pltpu.make_async_remote_copy(
                 src_ref=slots.at[me, pl.ds(0, 1), :],
                 dst_ref=slots.at[me, pl.ds(0, 1), :],
-                send_sem=sum_send.at[axis, d],
-                recv_sem=sum_recv.at[axis, d],
+                send_sem=sum_send.at[axis * ngx + d],
+                recv_sem=sum_recv.at[axis * ngx + d],
                 device_id=peer(axis, d),
                 device_id_type=pl.DeviceIdType.MESH,
             )
@@ -530,20 +532,19 @@
     lax.fori_loop(nrow // 16, nrow // 8, merge, 0, unroll=4)
     for copy in y_copies:
         copy.wait()
-    total = sum(gather_y[i, 0:1, :] for i in range(ngy))
-    cells = nrow * ngx * ncol * ngy
-    low = lax.broadcasted_iota(jnp.int32, (1, LANES), 1) < half
-    out_res[0, 0] = jnp.sum(jnp.where(low, total, 0.0)) * (1.0 / cells)
-    out_kin[0, 0] = jnp.sum(jnp.where(low, 0.0, total)) * (0.5 * time_step / 4.0 / cells)
-
-
-def store_kernel(vel, stress, residual, kinetic, out_vel, out_str, out_res, out_kin, sem):
+    out_sum[...] = sum(gather_y[i, 0:1, :] for i in range(ngy))
+
+
+def store_kernel(cells, vel, stress, total, out_vel, out_str, out_res, out_kin, res, kin, sem):
     copies = [pltpu.make_async_copy(vel.at[i], out_vel.at[i], sem.at[i]) for i in range(2)]
     copies += [pltpu.make_async_copy(stress.at[i], out_str.at[i], sem.at[2 + i]) for i in range(3)]
+    low = lax.broadcasted_iota(jnp.int32, (1, LANES), 1) < LANES // 2
+    both = total[...]
+    res[...] = jnp.sum(jnp.where(low, both, 0.0), axis=1, keepdims=True) * (1.0 / cells)
+    kin[...] = jnp.sum(jnp.where(low, 0.0, both), axis=1, keepdims=True) * (0.5 * time_step / 4.0 / cells)
+    copies += [pltpu.make_async_copy(res, out_res, sem.at[5]), pltpu.make_async_copy(kin, out_kin, sem.at[6])]
     for copy in copies:
         copy.start()
-    out_res[0, 0] = residual[0, 0]
-    out_kin[0, 0] = kinetic[0, 0]
     for copy in copies:
         copy.wait()
 
@@ -556,18 +557,16 @@
     vmem = pltpu.VMEM
     any_spec = pl.BlockSpec(memory_space=pl.ANY)
     vmem_spec = pl.BlockSpec(memory_space=pltpu.VMEM)
-    smem_spec = pl.BlockSpec(memory_space=pltpu.SMEM)
     ngx, ngy = lax.axis_size(GX), lax.axis_size(GY)
-    new_velocity, new_stress, residual, kinetic = pl.pallas_call(
+    new_velocity, new_stress, total = pl.pallas_call(
         main_kernel,
         out_shape=(
             vmem(velocity.shape, F32),
             vmem(stress.shape, F32),
-            jax.ShapeDtypeStruct((1, 1), F32),
-            jax.ShapeDtypeStruct((1, 1), F32),
+            vmem((1, LANES), F32),
         ),
         in_specs=[any_spec] * 8,
-        out_specs=(vmem_spec, vmem_spec, smem_spec, smem_spec),
+        out_specs=(vmem_spec, vmem_spec, vmem_spec),
         scratch_shapes=[
             vmem((2, nblk, pad, LANES), F32),
             vmem((3, nrow, ncol), F32),
@@ -592,11 +591,11 @@
             vmem((row_blks, LANES, LANES), F32),
             vmem((ngx, 8, LANES), F32),
             vmem((ngy, 8, LANES), F32),
-            pltpu.SemaphoreType.DMA((nblk + 7, CHUNKS)),
+            pltpu.SemaphoreType.DMA((nblk + 7, AHEAD + 1)),
             pltpu.SemaphoreType.DMA((2, 2)),
             pltpu.SemaphoreType.DMA((2, 2)),
-            pltpu.SemaphoreType.DMA((2, max(ngx, ngy))),
-            pltpu.SemaphoreType.DMA((2, max(ngx, ngy))),
+            pltpu.SemaphoreType.DMA((ngx + ngy,)),
+            pltpu.SemaphoreType.DMA((ngx + ngy,)),
         ],
         compiler_params=pltpu.CompilerParams(
             collective_id=0, has_side_effects=True, vmem_limit_bytes=57 * 1024 * 1024
@@ -604,19 +603,19 @@
         name="subcycles",
     )(velocity, stress, strength, ice_mass, wind_stress, current, ice_mask, open_water)
     new_velocity, new_stress, residual, kinetic = pl.pallas_call(
-        store_kernel,
+        functools.partial(store_kernel, nrow * ngx * ncol * ngy),
         out_shape=(
             jax.ShapeDtypeStruct(velocity.shape, F32),
             jax.ShapeDtypeStruct(stress.shape, F32),
             jax.ShapeDtypeStruct((1, 1), F32),
             jax.ShapeDtypeStruct((1, 1), F32),
         ),
-        in_specs=[vmem_spec, vmem_spec, smem_spec, smem_spec],
-        out_specs=(any_spec, any_spec, smem_spec, smem_spec),
-        scratch_shapes=[pltpu.SemaphoreType.DMA((5,))],
+        in_specs=[vmem_spec] * 3,
+        out_specs=(any_spec,) * 4,
+        scratch_shapes=[vmem((1, 1), F32), vmem((1, 1), F32), pltpu.SemaphoreType.DMA((7,))],
         compiler_params=pltpu.CompilerParams(vmem_limit_bytes=1024 * 1024),
         name="store",
-    )(new_velocity, new_stress, residual, kinetic)
+    )(new_velocity, new_stress, total)
     return new_velocity, new_stress, residual.reshape(()), kinetic.reshape(())
 
 

time: 40.4 us -> 36.9 us (0.913)
  Pallas kernels: 39.6 us -> 36.1 us
    pallas_call x1, Pallas kernels: 4.18 us -> 2.42 us  [per_device(): pl.pallas_call(functools.partial(store_kernel, nrow * ngx * ncol * ngy),...]
    pallas_call x1, Pallas kernels: 35.4 us -> 33.7 us  [per_device(): pl.pallas_call(main_kernel, out_shape=(vmem(velocity.shape, F32), vmem(st...]
where the time goes in v3:
time: 36.9 us; the launch traced here: 36.8 us
  Pallas kernels  36.1 us (98%)
  between operations  0.64 us (2%)
    pallas_call x1, Pallas kernels, per_device(): pl.pallas_call(main_kernel, out_shape=(vmem(velocity.shape, F32), vmem(st...  33.7 us
    pallas_call x1, Pallas kernels, per_device(): pl.pallas_call(functools.partial(store_kernel, nrow * ngx * ncol * ngy),...  2.42 us

profile of v3, /device:TPU:1, one launch (start us, length us, event | category | flops | bytes accessed | tf_op | source)
XLA Modules:
  0.0 36.8 jit_solution(5096265235229907820)
XLA Ops:
  0.6 33.7 %subcycles.1 = (f32[2,512,512]{2,1,0:T(8,128)S(1)}, f32[3,512,512]{2,1,0:T(8,128)S(1)}, f32[1,128]{1,0:T(1,128)S(1)}) custom-call(f32[2,512,512]{2,1,0:T(8,128)} %vel.1, f32[3,512,512]{2,1,0:T(8,128)} %stress.1, f32[512,512]{1,0:T(8,128)} %strength.1, f32[512,512]{1,0:T(8,128)} %mass.1, f32[2,512,512]{2,1,0:T(8,128)} %wind.1, f32[2,512,512]{2,1,0:T(8,128)} %current.1, ...), custom_call_target="tpu_custom_call" | custom-call | tf_op jit(solution)/shard_map/subcycles/pallas_call | solution.py:561
  34.4 2.4 %store.1 = (f32[2,512,512]{2,1,0:T(8,128)}, f32[3,512,512]{2,1,0:T(8,128)}, f32[1,1]{1,0:T(1,128)}, f32[1,1]{1,0:T(1,128)}) custom-call(f32[2,512,512]{2,1,0:T(8,128)S(1)} %get-tuple-element.11.vel, f32[3,512,512]{2,1,0:T(8,128)S(1)} %get-tuple-element.12.stress, f32[1,128]{1,0:T(1,128)S(1)} %get-tuple-element.13.total), custom_call_target="tpu_custom_call" | custom-call | tf_op jit(solution)/shard_map/store/pallas_call | solution.py:605
